TPU v7x, 512 devices: a whole 4x8x8 slice. The times are simulated.
512 devices in a mesh: gx: 32 (over y_hi, x, core), gy: 16 (over y_lo, z).
Axes of the slice: x: 4, y: 8 (y_hi: 4, y_lo: 2; y = y_hi * 2 + y_lo), z: 8, core: 2. Of those that a mesh axis runs over, the one named last changes fastest.
Arguments:
- node_values: bfloat16 [96, 48, 128, 256], P('gx', 'gy'), may hold values from -6 to 6
- fit_ops: bfloat16 [32, 16, 8, 320, 300], P('gx', 'gy'), may hold values from -0.0034179688 to 0.0034179688
- node_xyz: float32 [32, 16, 8, 3, 300], P('gx', 'gy'), may hold values from -6 to 6
- patch_nodes: int32 [32, 16, 8, 300], P('gx', 'gy'), may hold values from 0 to 3199, as said below
- patch_valid: int32 [32, 16, 8], P('gx', 'gy'), may hold values from 160 to 300
- patch_cell: int32 [32, 16, 8, 3], P('gx', 'gy'), may hold values from 0 to 11, as said below
- patch_radius: float32 [32, 16, 8], P('gx', 'gy'), may hold values from 3 to 6
- cell_scale: float32 [384, 192, 8], P('gx', 'gy'), may hold values from 0.5 to 2
Outputs:
- velocity: bfloat16 [384, 192, 8, 256], P('gx', 'gy')
Inputs may be any that keep to these rules, and one draw needn't show every extreme that they name: `patch_nodes`: an entry (a * 5 + b) * 128 + n names node n of subregion (a, b) among the 5 by 5 subregions around the patch's tile, whose own subregions are a, b = 1 to 3; a and b differ by at most one from the subregion 1 + (3 c0) // 12, 1 + (3 c1) // 12 that holds the patch's centre cell, and the subregion never lies outside the grid along the second horizontal dimension. `patch_cell`: the first entry is below 12, the second below 12, the third at most 4.
All inputs are finite; a program needn't handle non-finite values.
Results may differ from a plain program's by a relative error of at most 0.0085.
Values may be sent and summed in bfloat16 or wider, within the bound.
A program may use at most 64 MiB of HBM per device.

v0:
```python
import jax
import jax.numpy as jnp
import numpy as np
from jax import lax
from jax.sharding import PartitionSpec as P

EXPONENTS = (
    (0, 0, 0),
    (1, 0, 0),
    (0, 1, 0),
    (0, 0, 1),
    (2, 0, 0),
    (1, 1, 0),
    (1, 0, 1),
    (0, 2, 0),
    (0, 1, 1),
    (0, 0, 2),
    (3, 0, 0),
    (2, 1, 0),
    (2, 0, 1),
    (1, 2, 0),
    (1, 1, 1),
    (1, 0, 2),
    (0, 3, 0),
    (0, 2, 1),
    (0, 1, 2),
    (0, 0, 3),
)


def with_halo(x, sides, width, wrap):
    for axis, dim in sides:
        size, length = (lax.axis_size(axis), x.shape[dim])
        up = [(i, (i + 1) % size) for i in range(size if wrap else size - 1)]
        down = [(j, i) for i, j in up]
        last = lax.slice_in_dim(x, length - width, length, axis=dim)
        first = lax.slice_in_dim(x, 0, width, axis=dim)
        before = lax.ppermute(last, axis, up)
        after = lax.ppermute(first, axis, down)
        x = jnp.concatenate([before, x, after], axis=dim)
    return x


def stencil():
    across = np.arange(-4, 5).astype(np.float32)
    depth = np.arange(4).astype(np.float32) - 1.5
    first, second, third = np.meshgrid(across, across, depth, indexing="ij")
    return np.stack([first.ravel(), second.ravel(), third.ravel()], 1).astype(np.float32)


def patch_terms(gathered, operators, xyz, valid, radius):
    count = gathered.shape[0]
    fields = gathered.shape[2]
    slots = lax.broadcasted_iota(jnp.int32, gathered.shape[:2], 1)
    masked = jnp.where(
        (slots < valid[:, None])[:, :, None], gathered, jnp.zeros((), gathered.dtype)
    )
    coeffs = jnp.einsum(
        "pik,pkf->pif", operators, masked, preferred_element_type=jnp.float32
    ).astype(jnp.bfloat16)
    points = jnp.asarray(stencil())
    inverse = 1.0 / radius
    squared = jnp.zeros((count, points.shape[0], xyz.shape[2]), jnp.float32)
    for component in range(3):
        offset = points[None, :, component, None] - xyz[:, None, component, :]
        squared = squared + offset * offset
    scaled = squared * (inverse * inverse)[:, None, None]
    kernel = scaled * jnp.sqrt(scaled)
    unit_points = points[None, :, :] * inverse[:, None, None]
    powers = [
        jnp.ones_like(unit_points),
        unit_points,
        unit_points * unit_points,
        unit_points * unit_points * unit_points,
    ]
    monomials = [
        powers[first][..., 0] * powers[second][..., 1] * powers[third][..., 2]
        for first, second, third in EXPONENTS
    ]
    design = jnp.concatenate([kernel, jnp.stack(monomials, -1)], -1).astype(jnp.bfloat16)
    values = jnp.einsum("pmi,pif->pmf", design, coeffs, preferred_element_type=jnp.float32)
    distance = jnp.sqrt(jnp.sum(points * points, 1))[None, :] * inverse[:, None]
    blend = jnp.maximum(1.0 - distance, 0.0) ** 4 * (4.0 * distance + 1.0)
    terms = values * blend[:, :, None]
    return terms.reshape(count, 9, 9, 4, fields)


def one_hot_place(starts, cells_total, offsets):
    target = lax.broadcasted_iota(jnp.int32, (starts.shape[0], cells_total, offsets), 1)
    source = lax.broadcasted_iota(jnp.int32, (starts.shape[0], cells_total, offsets), 2)
    return jnp.where(target == starts[:, None, None] + source, 1.0, 0.0).astype(jnp.float32)


def fold_columns(buffer):
    inner_width = buffer.shape[0] - 8
    rims = jnp.concatenate([buffer[:4], buffer[inner_width + 4 :]], 0)
    arrived = with_halo(rims, (("gx", 0),), 4, True)
    inner = buffer[4 : inner_width + 4]
    inner = inner.at[:4].add(arrived[:4])
    inner = inner.at[inner_width - 4 :].add(arrived[12:16])
    return inner


def fold_rows(buffer):
    inner_width = buffer.shape[1] - 8
    rims = jnp.concatenate([buffer[:, :4], buffer[:, inner_width + 4 :]], 1)
    arrived = with_halo(rims, (("gy", 1),), 4, False)
    inner = buffer[:, 4 : inner_width + 4]
    inner = inner.at[:, :4].add(arrived[:, :4])
    inner = inner.at[:, inner_width - 4 :].add(arrived[:, 12:16])
    return inner


def local(
    node_values, fit_ops, node_xyz, patch_nodes, patch_valid, patch_cell, patch_radius, cell_scale
):
    fields = node_values.shape[3]
    subregion = node_values.shape[2]
    depth = width = 1
    widened = with_halo(node_values, (("gx", 0),), depth, True)
    neighbourhood = with_halo(widened, (("gy", 1),), depth, False)
    flat = neighbourhood.reshape(25 * subregion, fields)
    gathered = jnp.take(flat, patch_nodes[0, 0], axis=0)
    terms = patch_terms(
        gathered, fit_ops[0, 0], node_xyz[0, 0], patch_valid[0, 0], patch_radius[0, 0]
    )
    cells = patch_cell[0, 0]
    place_depth = one_hot_place(cells[:, 2], cell_scale.shape[2], 4)
    place_second = one_hot_place(cells[:, 1], cell_scale.shape[1] + 8, 9)
    place_first = one_hot_place(cells[:, 0], cell_scale.shape[0] + 8, 9)
    deep = jnp.einsum("pzc,pabcf->pabzf", place_depth, terms)
    across = jnp.einsum("pyb,pabzf->payzf", place_second, deep)
    buffer = jnp.einsum("pxa,payzf->xyzf", place_first, across)
    folded = fold_columns(fold_rows(buffer))
    return (cell_scale[..., None] * folded).astype(jnp.bfloat16)


def solution(mesh):
    placed = (
        P("gx", "gy", None, None),
        P("gx", "gy", None, None, None),
        P("gx", "gy", None, None, None),
        P("gx", "gy", None, None),
        P("gx", "gy", None),
        P("gx", "gy", None, None),
        P("gx", "gy", None),
        P("gx", "gy", None),
    )
    return jax.shard_map(
        local, mesh=mesh, in_specs=placed, out_specs=P("gx", "gy", None, None), check_vma=False
    )
```

profile of v0, /device:TPU:87, one launch (start us, length us, event | category | flops | bytes accessed | tf_op | source)
XLA Modules:
  0.0 118.5 jit_solution(5390249157004553345)
XLA Ops:
  0.0 1.2 fusion.74
  1.2 5.9 %collective-permute-start = (bf16[1,3,128,256]{3,2,1,0:T(8,128)(2,1)S(1)}, bf16[1,3,128,256]{3,2,1,0:T(8,128)(2,1)S(1)}, u32[]{:S(2)}, u32[]{:S(2)}) collective-permute-start(bf16[1,3,128,256]{3,2,1,0:T(8,128)(2,1)S(1)} %get-tuple-element.62), channel_id=1, source_target_pairs={{0,16},{16,32},{32,48},{48,64},{64,80},{80,96},{96,112},{112,128},... | collective-permute-start | bytes 589832 | tf_op jit(solution)/shard_map/ppermute | solution.py:38
  7.1 1.9 %collective-permute-start.1 = (bf16[1,3,128,256]{3,2,1,0:T(8,128)(2,1)S(1)}, bf16[1,3,128,256]{3,2,1,0:T(8,128)(2,1)S(1)}, u32[]{:S(2)}, u32[]{:S(2)}) collective-permute-start(bf16[1,3,128,256]{3,2,1,0:T(8,128)(2,1)S(1)} %get-tuple-element.61), channel_id=1, source_target_pairs={{16,0},{32,16},{48,32},{64,48},{80,64},{96,80},{112,96},{128,112},... | collective-permute-start | bytes 589832 | tf_op jit(solution)/shard_map/ppermute | solution.py:39
  9.0 0.7 fusion.70
  9.7 0.8 fusion.43
  10.5 0.1 multiply_convert_fusion.2
  10.7 0.7 slice_bitcast_fusion.2
  11.4 0.7 compare_select_fusion
  12.1 0.1 reshape.264
  12.2 0.8 fusion.55
  13.0 0.7 copy.52
  13.7 4.0 %fusion.7 = bf16[8,324,300]{1,2,0:T(8,128)(2,1)} fusion(f32[8]{0:T(128)S(1)} %get-tuple-element.53, f32[8,300]{1,0:T(8,128)S(1)} %get-tuple-element.76, f32[324]{0:T(512)} %constant.151, f32[8,300]{1,0:T(8,128)S(1)} %get-tuple-element.77, f32[324]{0:T(512)} %constant.149, f32[8,300]{1,0:T(8,128)S(1)} %get-tuple-element.75, f32[324]{0:T(512)} %constant.147), kind=kLoop, calls=%fused_computation.7 | loop fusion | flops 8553600 | bytes 1587920 | tf_op jit(solution)/shard_map/convert
  17.7 12.5 %concatenate.19 = bf16[8,324,320]{1,2,0:T(8,128)(2,1)} concatenate(bf16[8,324,300]{1,2,0:T(8,128)(2,1)} %fusion.7, bf16[8,324,1]{1,2,0:T(2,128)(2,1)S(1)} %slice.239, bf16[8,324,3]{1,2,0:T(4,128)(2,1)S(1)} %get-tuple-element.83, bf16[8,324,1]{1,2,0:T(2,128)(2,1)S(1)} %get-tuple-element.74, bf16[8,324,1]{1,2,0:T(2,128)(2,1)S(1)} %multiply_convert_fusion.11, ...), dimensions={2} | concatenate | bytes 3317760 | tf_op jit(solution)/shard_map/concatenate | solution.py:80
  30.4 4.0 %collective-permute-start.2 = (bf16[5,1,128,256]{3,2,1,0:T(8,128)(2,1)S(1)}, bf16[5,1,128,256]{3,2,1,0:T(8,128)(2,1)S(1)}, u32[]{:S(2)}, u32[]{:S(2)}) collective-permute-start(bf16[5,1,128,256]{3,2,1,0:T(8,128)(2,1)S(1)} %get-tuple-element.59), channel_id=1, source_target_pairs={{0,1},{1,2},{2,3},{3,4},{4,5},{5,6},{6,7},{7,8},{8,9},{9,10},{10,1... | collective-permute-start | bytes 983048 | tf_op jit(solution)/shard_map/ppermute | solution.py:38
  34.4 1.9 %collective-permute-start.3 = (bf16[5,1,128,256]{3,2,1,0:T(8,128)(2,1)S(1)}, bf16[5,1,128,256]{3,2,1,0:T(8,128)(2,1)S(1)}, u32[]{:S(2)}, u32[]{:S(2)}) collective-permute-start(bf16[5,1,128,256]{3,2,1,0:T(8,128)(2,1)S(1)} %get-tuple-element.60), channel_id=1, source_target_pairs={{1,0},{2,1},{3,2},{4,3},{5,4},{6,5},{7,6},{8,7},{9,8},{10,9},{11,1... | collective-permute-start | bytes 983048 | tf_op jit(solution)/shard_map/ppermute | solution.py:39
  36.4 0.1 iota_compare_fusion
  36.4 4.5 %collective-permute-done.2 = bf16[5,1,128,256]{3,2,1,0:T(8,128)(2,1)S(1)} collective-permute-done((bf16[5,1,128,256]{3,2,1,0:T(8,128)(2,1)S(1)}, bf16[5,1,128,256]{3,2,1,0:T(8,128)(2,1)S(1)}, u32[]{:S(2)}, u32[]{:S(2)}) %collective-permute-start.2) | collective-permute-done | bytes 327712 | tf_op jit(solution)/shard_map/ppermute | solution.py:38
  40.9 4.4 %collective-permute-done.3 = bf16[5,1,128,256]{3,2,1,0:T(8,128)(2,1)S(1)} collective-permute-done((bf16[5,1,128,256]{3,2,1,0:T(8,128)(2,1)S(1)}, bf16[5,1,128,256]{3,2,1,0:T(8,128)(2,1)S(1)}, u32[]{:S(2)}, u32[]{:S(2)}) %collective-permute-start.3) | collective-permute-done | bytes 327712 | tf_op jit(solution)/shard_map/ppermute | solution.py:39
  45.2 0.2 pad_maximum_fusion
  45.4 8.1 %gather_fusion = bf16[2400,256]{1,0:T(8,128)(2,1)} fusion(bf16[3200,256]{1,0:T(8,128)(2,1)S(1)} %bitcast.55, s32[3072]{0:T(1024)S(1)} %pad_clamp_fusion), kind=kCustom, calls=%fused_computation | custom fusion | bytes 2467200 | tf_op jit(solution)/shard_map/jit(_take)/gather | solution.py:123
  53.6 2.2 %reshape.263 = bf16[8,300,256]{2,1,0:T(8,128)(2,1)} reshape(bf16[2400,256]{1,0:T(8,128)(2,1)} %gather_fusion) | data formatting | bytes 2457600 | tf_op jit(solution)/shard_map/jit(_take)/gather | solution.py:123
  55.8 4.3 %convolution_multiply_fusion = bf16[8,324,256]{2,1,0:T(8,128)(2,1)S(1)} fusion(bf16[8,324,320]{1,2,0:T(8,128)(2,1)} %concatenate.19, bf16[8,320,300]{1,0,2:T(8,128)(2,1)S(1)} %bitcast.54, f32[8,324]{1,0:T(8,128)S(1)} %fusion.55, bf16[8,300,256]{2,1,0:T(8,128)(2,1)} %reshape.263, pred[8,300]{1,0:T(8,128)(4,1)S(1)} %get-tuple-element.92, ...), kind=kOutput, calls=%fused_computation.14 | convolution fusion | flops 821100544 | bytes 5765952 | tf_op jit(solution)/shard_map/pmi,pif->pmf/dot_general | solution.py:81
  60.1 0.3 copy.17
  60.4 1.0 fusion.10
  61.4 2.1 %fusion.4 = bf16[8,9,20,8,256]{4,2,3,1,0:T(8,128)(2,1)S(1)} fusion(bf16[8,9,9,8,256]{4,3,2,1,0:T(8,128)(2,1)S(1)} %fusion.10, s32[8]{0:T(128)S(1)} %get-tuple-element.86), kind=kOutput, calls=%fused_computation.5 | convolution fusion | flops 53088480 | bytes 8552480 | tf_op jit(solution)/shard_map/pyb,pabzf->payzf/dot_general | solution.py:132
  63.5 6.4 %fusion.13 = f32[20,20,8,256]{3,0,2,1:T(8,128)S(1)} fusion(bf16[8,9,20,8,256]{4,2,3,1,0:T(8,128)(2,1)S(1)} %fusion.4, s32[8]{0:T(128)S(1)} %get-tuple-element.85), kind=kOutput, calls=%fused_computation.11 | convolution fusion | flops 117969120 | bytes 9175072 | tf_op jit(solution)/shard_map/pxa,payzf->xyzf/dot_general | solution.py:133
  69.9 0.1 fusion.71
  70.0 0.2 copy.21
  70.2 5.2 %collective-permute-start.4 = (f32[20,4,8,256]{3,2,1,0:T(8,128)S(1)}, f32[20,4,8,256]{3,2,1,0:T(8,128)S(1)}, u32[]{:S(2)}, u32[]{:S(2)}) collective-permute-start(f32[20,4,8,256]{3,2,1,0:T(8,128)S(1)} %copy.21), channel_id=1, source_target_pairs={{0,1},{1,2},{2,3},{3,4},{4,5},{5,6},{6,7},{7,8},{8,9},{9,10},{10,1... | collective-permute-start | bytes 1966088 | tf_op jit(solution)/shard_map/ppermute | solution.py:38
  75.4 0.2 copy.23
  75.6 1.9 %collective-permute-start.5 = (f32[20,4,8,256]{3,2,1,0:T(8,128)S(1)}, f32[20,4,8,256]{3,2,1,0:T(8,128)S(1)}, u32[]{:S(2)}, u32[]{:S(2)}) collective-permute-start(f32[20,4,8,256]{3,2,1,0:T(8,128)S(1)} %copy.23), channel_id=1, source_target_pairs={{1,0},{2,1},{3,2},{4,3},{5,4},{6,5},{7,6},{8,7},{9,8},{10,9},{11,1... | collective-permute-start | bytes 1966088 | tf_op jit(solution)/shard_map/ppermute | solution.py:39
  77.5 0.3 slice.282
  77.8 12.1 %collective-permute-done.4 = f32[20,4,8,256]{3,2,1,0:T(8,128)S(1)} collective-permute-done((f32[20,4,8,256]{3,2,1,0:T(8,128)S(1)}, f32[20,4,8,256]{3,2,1,0:T(8,128)S(1)}, u32[]{:S(2)}, u32[]{:S(2)}) %collective-permute-start.4) | collective-permute-done | bytes 655392 | tf_op jit(solution)/shard_map/ppermute | solution.py:38
  89.9 0.4 fusion.32
  90.3 5.1 %collective-permute-done.5 = f32[20,4,8,256]{3,2,1,0:T(8,128)S(1)} collective-permute-done((f32[20,4,8,256]{3,2,1,0:T(8,128)S(1)}, f32[20,4,8,256]{3,2,1,0:T(8,128)S(1)}, u32[]{:S(2)}, u32[]{:S(2)}) %collective-permute-start.5) | collective-permute-done | bytes 655392 | tf_op jit(solution)/shard_map/ppermute | solution.py:39
  95.4 0.6 fusion.31
  96.0 1.4 %copy-done.1 = f32[20,12,8,256]{3,0,2,1:T(8,128)} copy-done((f32[20,12,8,256]{3,0,2,1:T(8,128)}, f32[20,12,8,256]{3,0,2,1:T(8,128)S(1)}, u32[]{:S(2)}) %copy-start.1) | copy-done | bytes 1966104
  97.5 0.1 fusion.72
  97.6 1.9 %collective-permute-start.6 = (f32[4,12,8,256]{3,0,2,1:T(4,128)S(1)}, f32[4,12,8,256]{3,0,2,1:T(4,128)S(1)}, u32[]{:S(2)}, u32[]{:S(2)}) collective-permute-start(f32[4,12,8,256]{3,0,2,1:T(4,128)S(1)} %get-tuple-element.58), channel_id=1, source_target_pairs={{0,16},{16,32},{32,48},{48,64},{64,80},{80,96},{96,112},{112,128},... | collective-permute-start | bytes 1179656 | tf_op jit(solution)/shard_map/ppermute | solution.py:38
  99.5 2.6 %collective-permute-start.7 = (f32[4,12,8,256]{3,0,2,1:T(4,128)S(1)}, f32[4,12,8,256]{3,0,2,1:T(4,128)S(1)}, u32[]{:S(2)}, u32[]{:S(2)}) collective-permute-start(f32[4,12,8,256]{3,0,2,1:T(4,128)S(1)} %get-tuple-element.57), channel_id=1, source_target_pairs={{16,0},{32,16},{48,32},{64,48},{80,64},{96,80},{112,96},{128,112},... | collective-permute-start | bytes 1179656 | tf_op jit(solution)/shard_map/ppermute | solution.py:39
  102.1 0.1 copy.15
  102.3 1.9 %slice.287 = f32[12,12,8,256]{3,0,2,1:T(8,128)S(1)} slice(f32[20,12,8,256]{3,0,2,1:T(8,128)} %copy-done.1), slice={[4:16], [0:12], [0:8], [0:256]} | slice | bytes 2359296 | tf_op jit(solution)/shard_map/slice | solution.py:98
  104.2 4.2 %collective-permute-done.6 = f32[4,12,8,256]{3,0,2,1:T(4,128)S(1)} collective-permute-done((f32[4,12,8,256]{3,0,2,1:T(4,128)S(1)}, f32[4,12,8,256]{3,0,2,1:T(4,128)S(1)}, u32[]{:S(2)}, u32[]{:S(2)}) %collective-permute-start.6) | collective-permute-done | bytes 393248 | tf_op jit(solution)/shard_map/ppermute | solution.py:38
  108.3 1.3 %fusion.38 = f32[12,12,8,256]{3,0,2,1:T(8,128)S(1)} fusion(f32[12,12,8,256]{3,0,2,1:T(8,128)S(1)} %slice.287, f32[4,12,8,256]{3,0,2,1:T(4,128)S(1)} %collective-permute-done.6, f32[20,12,8,256]{3,0,2,1:T(8,128)} %copy-done.1), kind=kLoop, calls=%fused_computation.31 | loop fusion | flops 98304 | bytes 1179648 | tf_op jit(solution)/shard_map/scatter-add | solution.py:99
  109.7 7.4 %collective-permute-done.7 = f32[4,12,8,256]{3,0,2,1:T(4,128)S(1)} collective-permute-done((f32[4,12,8,256]{3,0,2,1:T(4,128)S(1)}, f32[4,12,8,256]{3,0,2,1:T(4,128)S(1)}, u32[]{:S(2)}, u32[]{:S(2)}) %collective-permute-start.7) | collective-permute-done | bytes 393248 | tf_op jit(solution)/shard_map/ppermute | solution.py:39
  117.0 0.2 fusion.37
  117.3 0.3 multiply_convert_fusion
  117.5 1.0 copy.25
  (22 shorter events, 0.2 us)
Async XLA Ops:
  0.0 55.8 %copy-start = (bf16[1,1,8,320,300]{3,2,4,1,0:T(8,128)(2,1)S(1)}, bf16[1,1,8,320,300]{3,2,4,1,0:T(8,128)(2,1)}, u32[]{:S(2)}) copy-start(bf16[1,1,8,320,300]{3,2,4,1,0:T(8,128)(2,1)} %param.18) | copy-start | bytes 4608004
  1.2 29.0 %collective-permute-start = (bf16[1,3,128,256]{3,2,1,0:T(8,128)(2,1)S(1)}, bf16[1,3,128,256]{3,2,1,0:T(8,128)(2,1)S(1)}, u32[]{:S(2)}, u32[]{:S(2)}) collective-permute-start(bf16[1,3,128,256]{3,2,1,0:T(8,128)(2,1)S(1)} %get-tuple-element.62), channel_id=1, source_target_pairs={{0,16},{16,32},{32,48},{48,64},{64,80},{80,96},{96,112},{112,128},... | collective-permute-start | bytes 589832 | tf_op jit(solution)/shard_map/ppermute | solution.py:38
  7.1 23.2 %collective-permute-start.1 = (bf16[1,3,128,256]{3,2,1,0:T(8,128)(2,1)S(1)}, bf16[1,3,128,256]{3,2,1,0:T(8,128)(2,1)S(1)}, u32[]{:S(2)}, u32[]{:S(2)}) collective-permute-start(bf16[1,3,128,256]{3,2,1,0:T(8,128)(2,1)S(1)} %get-tuple-element.61), channel_id=1, source_target_pairs={{16,0},{32,16},{48,32},{64,48},{80,64},{96,80},{112,96},{128,112},... | collective-permute-start | bytes 589832 | tf_op jit(solution)/shard_map/ppermute | solution.py:39
  17.7 12.5 %copy-start.2 = (bf16[3,3,128,256]{3,2,1,0:T(8,128)(2,1)S(1)}, bf16[3,3,128,256]{3,2,1,0:T(8,128)(2,1)}, u32[]{:S(2)}) copy-start(bf16[3,3,128,256]{3,2,1,0:T(8,128)(2,1)} %param.17) | copy-start | bytes 1769476
  30.2 6.1 %copy-start.4 = (s32[1,1,8,300]{3,2,1,0:T(8,128)S(1)}, s32[1,1,8,300]{3,2,1,0:T(8,128)}, u32[]{:S(2)}) copy-start(s32[1,1,8,300]{3,2,1,0:T(8,128)} %param.20) | copy-start | bytes 28804
  30.2 6.1 %copy-start.5 = (s32[1,1,8]{2,1,0:T(1,128)S(1)}, s32[1,1,8]{2,1,0:T(1,128)}, u32[]{:S(2)}) copy-start(s32[1,1,8]{2,1,0:T(1,128)} %param.21) | copy-start | bytes 100
  30.4 10.5 %collective-permute-start.2 = (bf16[5,1,128,256]{3,2,1,0:T(8,128)(2,1)S(1)}, bf16[5,1,128,256]{3,2,1,0:T(8,128)(2,1)S(1)}, u32[]{:S(2)}, u32[]{:S(2)}) collective-permute-start(bf16[5,1,128,256]{3,2,1,0:T(8,128)(2,1)S(1)} %get-tuple-element.59), channel_id=1, source_target_pairs={{0,1},{1,2},{2,3},{3,4},{4,5},{5,6},{6,7},{7,8},{8,9},{9,10},{10,1... | collective-permute-start | bytes 983048 | tf_op jit(solution)/shard_map/ppermute | solution.py:38
  34.4 10.8 %collective-permute-start.3 = (bf16[5,1,128,256]{3,2,1,0:T(8,128)(2,1)S(1)}, bf16[5,1,128,256]{3,2,1,0:T(8,128)(2,1)S(1)}, u32[]{:S(2)}, u32[]{:S(2)}) collective-permute-start(bf16[5,1,128,256]{3,2,1,0:T(8,128)(2,1)S(1)} %get-tuple-element.60), channel_id=1, source_target_pairs={{1,0},{2,1},{3,2},{4,3},{5,4},{6,5},{7,6},{8,7},{9,8},{10,9},{11,1... | collective-permute-start | bytes 983048 | tf_op jit(solution)/shard_map/ppermute | solution.py:39
  70.2 19.7 %collective-permute-start.4 = (f32[20,4,8,256]{3,2,1,0:T(8,128)S(1)}, f32[20,4,8,256]{3,2,1,0:T(8,128)S(1)}, u32[]{:S(2)}, u32[]{:S(2)}) collective-permute-start(f32[20,4,8,256]{3,2,1,0:T(8,128)S(1)} %copy.21), channel_id=1, source_target_pairs={{0,1},{1,2},{2,3},{3,4},{4,5},{5,6},{6,7},{7,8},{8,9},{9,10},{10,1... | collective-permute-start | bytes 1966088 | tf_op jit(solution)/shard_map/ppermute | solution.py:38
  75.6 19.8 %collective-permute-start.5 = (f32[20,4,8,256]{3,2,1,0:T(8,128)S(1)}, f32[20,4,8,256]{3,2,1,0:T(8,128)S(1)}, u32[]{:S(2)}, u32[]{:S(2)}) collective-permute-start(f32[20,4,8,256]{3,2,1,0:T(8,128)S(1)} %copy.23), channel_id=1, source_target_pairs={{1,0},{2,1},{3,2},{4,3},{5,4},{6,5},{7,6},{8,7},{9,8},{10,9},{11,1... | collective-permute-start | bytes 1966088 | tf_op jit(solution)/shard_map/ppermute | solution.py:39
  90.3 11.8 %copy-start.3 = (f32[12,12,8]{1,2,0:T(8,128)S(1)}, f32[12,12,8]{1,2,0:T(8,128)}, u32[]{:S(2)}) copy-start(f32[12,12,8]{1,2,0:T(8,128)} %param.24) | copy-start | bytes 13828
  96.0 1.4 %copy-start.1 = (f32[20,12,8,256]{3,0,2,1:T(8,128)}, f32[20,12,8,256]{3,0,2,1:T(8,128)S(1)}, u32[]{:S(2)}) copy-start(f32[20,12,8,256]{3,0,2,1:T(8,128)S(1)} %fusion.31) | copy-start | bytes 5898244
  97.6 10.7 %collective-permute-start.6 = (f32[4,12,8,256]{3,0,2,1:T(4,128)S(1)}, f32[4,12,8,256]{3,0,2,1:T(4,128)S(1)}, u32[]{:S(2)}, u32[]{:S(2)}) collective-permute-start(f32[4,12,8,256]{3,0,2,1:T(4,128)S(1)} %get-tuple-element.58), channel_id=1, source_target_pairs={{0,16},{16,32},{32,48},{48,64},{64,80},{80,96},{96,112},{112,128},... | collective-permute-start | bytes 1179656 | tf_op jit(solution)/shard_map/ppermute | solution.py:38
  99.5 17.5 %collective-permute-start.7 = (f32[4,12,8,256]{3,0,2,1:T(4,128)S(1)}, f32[4,12,8,256]{3,0,2,1:T(4,128)S(1)}, u32[]{:S(2)}, u32[]{:S(2)}) collective-permute-start(f32[4,12,8,256]{3,0,2,1:T(4,128)S(1)} %get-tuple-element.57), channel_id=1, source_target_pairs={{16,0},{32,16},{48,32},{64,48},{80,64},{96,80},{112,96},{128,112},... | collective-permute-start | bytes 1179656 | tf_op jit(solution)/shard_map/ppermute | solution.py:39
where the time goes:
time: 120 us; the launch traced here: 119 us
  waiting for transfers between devices  37.5 us (31%)
  local copies, waits for them, and re-layouts  31.4 us (26%)
  starting transfers between devices  25.4 us (21%)
  matrix products  13.7 us (11%)
  other arithmetic  10.2 us (8%)
    ppermute x4, waiting for transfers between devices, with_halo(): before = lax.ppermute(last, axis, up)  20.7 us
    ppermute x4, starting transfers between devices, with_halo(): before = lax.ppermute(last, axis, up)  17 us
    ppermute x4, waiting for transfers between devices, with_halo(): after = lax.ppermute(first, axis, down)  16.8 us
    concatenate x1, local copies, waits for them, and re-layouts, patch_terms(): jnp.concatenate([kernel, jnp.stack(monomials, -1)], -1).astype(jnp.bfloat16)  12.5 us
    gather x2, local copies, waits for them, and re-layouts, local(): gathered = jnp.take(flat, patch_nodes[0, 0], axis=0)  10.4 us
    ppermute x4, starting transfers between devices, with_halo(): after = lax.ppermute(first, axis, down)  8.37 us
    dot_general x1, matrix products, local(): buffer = jnp.einsum('pxa,payzf->xyzf', place_first, across)  6.37 us
    another operation x4, other arithmetic  4.94 us
  transfers between devices with their start and end apart: 8, of which 6 were waited for; matrix products, arithmetic and copies ran while one was open for 22% of the time, Pallas kernels for 0%

commit v1 on v0

v1 whole, which is shorter than its diff:
```python
import functools

import jax
import jax.numpy as jnp
from jax import lax
from jax.experimental import pallas as pl
from jax.experimental.pallas import tpu as pltpu
from jax.sharding import PartitionSpec as P

EXPONENTS = (
    (0, 0, 0),
    (1, 0, 0),
    (0, 1, 0),
    (0, 0, 1),
    (2, 0, 0),
    (1, 1, 0),
    (1, 0, 1),
    (0, 2, 0),
    (0, 1, 1),
    (0, 0, 2),
    (3, 0, 0),
    (2, 1, 0),
    (2, 0, 1),
    (1, 2, 0),
    (1, 1, 1),
    (1, 0, 2),
    (0, 3, 0),
    (0, 2, 1),
    (0, 1, 2),
    (0, 0, 3),
)

K = 300
KS = 304
KP = 320
KL = 384
NSUB = 128
PATCHES = 8
SLAB = 48
BF = jnp.bfloat16
F32 = jnp.float32


def remote(src, dst, send, recv, axis, target):
    return pltpu.make_async_remote_copy(
        src_ref=src,
        dst_ref=dst,
        send_sem=send,
        recv_sem=recv,
        device_id={axis: target},
        device_id_type=pl.DeviceIdType.MESH,
    )


def kernel(
    nx,
    ny,
    nodes_hbm,
    fit_hbm,
    xyz_hbm,
    idx_hbm,
    scale_hbm,
    cell_ref,
    valid_ref,
    radius_ref,
    out_ref,
    nbr,
    fit_v,
    xyz_v,
    idx_v,
    scale_v,
    xyz_p,
    idx_b,
    ops_f,
    design,
    weights,
    onehot,
    place,
    slabs,
    acc,
    sxc,
    sxm,
    sz,
    rxc,
    rxm,
    rz,
    local_sem,
    hz_send,
    hz_recv,
    hx_send,
    hx_recv,
    hf_send,
    hf_recv,
    cc_send,
    cc_recv,
    cm_send,
    cm_recv,
    cz_send,
    cz_recv,
):
    gx, gy = lax.axis_index("gx"), lax.axis_index("gy")
    left, right = lax.rem(gx + nx - 1, nx), lax.rem(gx + 1, nx)
    sides_x = (left, right)
    has = (gy > 0, gy < ny - 1)
    sides_y = (jnp.maximum(gy - 1, 0), jnp.minimum(gy + 1, ny - 1))

    barrier = pltpu.get_barrier_semaphore()
    for side in sides_x:
        pl.semaphore_signal(
            barrier, inc=1, device_id={"gx": side}, device_id_type=pl.DeviceIdType.MESH
        )
    for d in range(2):

        @pl.when(has[d])
        def _():
            pl.semaphore_signal(
                barrier,
                inc=1,
                device_id={"gy": sides_y[d]},
                device_id_type=pl.DeviceIdType.MESH,
            )

    fetches = [
        pltpu.make_async_copy(idx_hbm, idx_v, local_sem.at[0]),
        pltpu.make_async_copy(xyz_hbm, xyz_v, local_sem.at[1]),
        pltpu.make_async_copy(fit_hbm, fit_v, local_sem.at[2]),
        pltpu.make_async_copy(scale_hbm, scale_v, local_sem.at[3]),
    ]
    for a in range(3):
        fetches.append(
            pltpu.make_async_copy(
                nodes_hbm.at[a], nbr.at[a + 1, pl.ds(1, 3)], local_sem.at[4 + a]
            )
        )
    for fetch in fetches:
        fetch.start()
    waits = 2 + jnp.where(gy > 0, 1, 0) + jnp.where(gy < ny - 1, 1, 0)
    pl.semaphore_wait(barrier, waits)

    def halo_y(d, a):
        return remote(
            nodes_hbm.at[a, 2 * d],
            nbr.at[a + 1, 4 - 4 * d],
            hz_send.at[d, a],
            hz_recv.at[d, a],
            "gy",
            sides_y[d],
        )

    def halo_x(d):
        return remote(
            nodes_hbm.at[2 * d],
            nbr.at[4 - 4 * d, pl.ds(1, 3)],
            hx_send.at[d],
            hx_recv.at[d],
            "gx",
            sides_x[d],
        )

    def halo_corner(e, d):
        return remote(
            nbr.at[1 + 2 * d, 4 * e],
            nbr.at[4 - 4 * d, 4 * e],
            hf_send.at[e, d],
            hf_recv.at[e, d],
            "gx",
            sides_x[d],
        )

    for a in (0, 2, 1):
        for d in range(2):

            @pl.when(has[d])
            def _():
                halo_y(d, a).start()

    for d in range(2):
        halo_x(d).start()

    for e in range(2):

        @pl.when(jnp.logical_not(has[e]))
        def _():
            for a in range(5):
                nbr[a, 4 * e] = jnp.zeros(nbr.shape[2:], BF)
            rz[1 - e] = jnp.zeros(rz.shape[1:], BF)

    fetches[0].wait()
    fetches[1].wait()
    xyz_p[...] = jnp.zeros(xyz_p.shape, F32)
    xyz_p[:, :, 0:K] = xyz_v[...]
    index = jnp.concatenate(
        [idx_v[...].astype(F32), jnp.zeros((PATCHES, KL - K), F32)], 1
    )
    columns = jnp.transpose(index)
    for p in range(PATCHES):
        idx_b[p] = jnp.broadcast_to(columns[0:KS, p : p + 1], (KS, 128)).astype(jnp.int32)

    for p in range(PATCHES):
        slabs[p, 9] = jnp.zeros((SLAB, slabs.shape[3]), BF)

    lane = lax.broadcasted_iota(jnp.int32, (1, KL), 1)
    owner, within = lane // SLAB, lane % SLAB
    target = jnp.zeros((1, KL), jnp.int32)
    for p in range(PATCHES):
        start = cell_ref[0, 1, 0, p] * 8 + cell_ref[0, 2, 0, p]
        target = jnp.where(owner == p, start, target)
    target = target + (within // 4) * 8 + within % 4
    target = jnp.where(within < 36, target, -1)
    rows = lax.broadcasted_iota(jnp.int32, (160, KL), 0)
    place[...] = jnp.where(rows == target, 1.0, 0.0).astype(BF)

    fetches[2].wait()
    for t in range(3):
        ops_f[t, K * 8 : KS * 8, :] = jnp.zeros(((KS - K) * 8, 128), F32)
    ops_f[2, :, 64:128] = jnp.zeros((KS * 8, 64), F32)

    def widen(i, carry):
        block = fit_v[pl.ds(i * 20, 20)].astype(F32).reshape(160, KP)
        at = pl.multiple_of(i * 160, 8)
        ops_f[0, pl.ds(at, 160), :] = block[:, 0:128]
        ops_f[1, pl.ds(at, 160), :] = block[:, 128:256]
        ops_f[2, pl.ds(at, 160), 0:64] = block[:, 256:320]
        return carry

    lax.fori_loop(0, K // 20, widen, 0)

    def prepare(p, carry):
        inverse = 1.0 / jnp.full((1, 128), radius_ref[0, 0, p], F32)
        inverse3 = jnp.concatenate([inverse] * 3, 1)
        x = xyz_p[0, pl.ds(p, 1), :] * inverse3
        y = xyz_p[1, pl.ds(p, 1), :] * inverse3
        z = xyz_p[2, pl.ds(p, 1), :] * inverse3
        row = lax.broadcasted_iota(jnp.int32, (SLAB, 128), 0)
        ey = (row // 4 - 4).astype(F32) * inverse
        ez = ((row % 4).astype(F32) - 1.5) * inverse
        ey3 = jnp.concatenate([ey] * 3, 1)
        ez3 = jnp.concatenate([ez] * 3, 1)
        away_yz = (ey3 - y) * (ey3 - y) + (ez3 - z) * (ez3 - z)
        flat = ey * ey + ez * ez
        tail = lax.broadcasted_iota(jnp.int32, (1, 128), 1) - (K - 256)

        def powers(base, which):
            result = jnp.zeros(jnp.broadcast_shapes(base.shape, (1, 128)), F32)
            raised = [jnp.ones_like(base), base, base * base, base * base * base]
            for power in range(4):
                hit = jnp.zeros((1, 128), jnp.bool_)
                for slot, exponent in enumerate(EXPONENTS):
                    if exponent[which] == power:
                        hit = hit | (tail == slot)
                result = jnp.where(hit, raised[power], result)
            return result

        mono_yz = powers(ey, 1) * powers(ez, 2)
        blends = []
        for i in range(9):
            ex = (i - 4) * inverse
            ex3 = jnp.concatenate([ex] * 3, 1)
            s = (ex3 - x) * (ex3 - x) + away_yz
            cubic = s * s * lax.rsqrt(jnp.maximum(s, 1e-30))
            mono = powers(ex, 0) * mono_yz
            last = jnp.where(tail < 0, cubic[:, 256:384], mono)
            design[SLAB * i : SLAB * i + SLAB, 0:256] = cubic[:, 0:256].astype(BF)
            design[SLAB * i : SLAB * i + SLAB, 256:384] = last.astype(BF)
            rho = jnp.sqrt(ex * ex + flat)
            rest = jnp.maximum(1.0 - rho, 0.0)
            rest = rest * rest
            blend = rest * rest * (4.0 * rho + 1.0)
            blends.append(jnp.where(row < 36, blend, 0.0))
        ops = jnp.concatenate(
            [ops_f[t, pl.ds(p, KS, stride=8), :].astype(BF) for t in range(3)], 1
        )
        ops = jnp.concatenate([ops, jnp.zeros((KL - KS, KL), BF)], 0)
        for i in range(9):
            w = lax.dot_general(
                design[SLAB * i : SLAB * i + SLAB, :],
                ops,
                (((1,), (1,)), ((), ())),
                preferred_element_type=F32,
            )
            weights[p, SLAB * i : SLAB * i + SLAB, :] = (
                w * jnp.concatenate([blends[i]] * 3, 1)
            ).astype(BF)

        entry = idx_b[p]
        sub = entry >> 7
        node = entry & 127
        a = (sub * 52) >> 8
        b = sub - 5 * a
        home = (cell_ref[0, 0, 0, p] // 4) * 3 + cell_ref[0, 1, 0, p] // 4
        block = a * 3 + b - home
        slot = lax.broadcasted_iota(jnp.int32, (KS, 128), 0)
        block = jnp.where(slot < valid_ref[0, 0, p], block, -1)
        match = jnp.where(
            node == lax.broadcasted_iota(jnp.int32, (KS, 128), 1), block, -1
        )
        for t in range(9):
            onehot[p, :, 128 * t : 128 * t + 128] = jnp.where(match == t, 1.0, 0.0).astype(BF)
        return carry

    lax.fori_loop(0, 4, prepare, 0)
    for e in range(2):

        @pl.when(has[e])
        def _():
            for d in range(2):
                halo_y(1 - e, 2 * d).wait_recv()
                halo_corner(e, d).start()

    lax.fori_loop(4, PATCHES, prepare, 0)

    for fetch in fetches[3:]:
        fetch.wait()
    for d in range(2):
        halo_x(d).wait_recv()
    for e in range(2):

        @pl.when(has[e])
        def _():
            halo_y(1 - e, 1).wait_recv()
            for d in range(2):
                halo_corner(e, d).wait_recv()

    def values(p, carry):
        home_x, home_y = cell_ref[0, 0, 0, p] // 4, cell_ref[0, 1, 0, p] // 4
        window = jnp.concatenate(
            [
                nbr[home_x + a, pl.ds(home_y, 3)].reshape(3 * NSUB, nbr.shape[3])
                for a in range(3)
            ],
            0,
        )
        samples = jnp.dot(onehot[p], window, preferred_element_type=F32).astype(BF)
        samples = jnp.concatenate(
            [samples, jnp.zeros((KL - KS, samples.shape[1]), BF)], 0
        )
        terms = jnp.dot(weights[p], samples, preferred_element_type=F32).astype(BF)
        slabs[p, 0:9] = terms.reshape(9, SLAB, terms.shape[1])
        return carry

    lax.fori_loop(0, PATCHES, values, 0)

    def reach(x):
        parts = []
        for p in range(PATCHES):
            at = x - cell_ref[0, 0, 0, p]
            at = jnp.where((at >= 0) & (at < 9), at, 9)
            parts.append(slabs[p, at])
        return jnp.dot(
            place[...], jnp.concatenate(parts, 0), preferred_element_type=F32
        )

    def send_corner(d, e):
        return remote(
            sxc.at[d, e], rxc.at[d, e], cc_send.at[d, e], cc_recv.at[d, e], "gx", sides_x[d]
        )

    def send_middle(d):
        return remote(sxm.at[d], rxm.at[d], cm_send.at[d], cm_recv.at[d], "gx", sides_x[d])

    def send_rows(d, part):
        return remote(
            sz.at[d, part],
            rz.at[d, part],
            cz_send.at[d, part],
            cz_recv.at[d, part],
            "gy",
            sides_y[d],
        )

    for d in range(2):

        def outer(i, carry):
            row = reach(16 * d + i)
            sxc[d, 0, i] = row[0:32].astype(BF)
            sxm[d, i] = row[32:128].astype(BF)
            sxc[d, 1, i] = row[128:160].astype(BF)
            return carry

        lax.fori_loop(0, 4, outer, 0)
        for e in range(2):
            send_corner(d, e).start()

    def inner(i, carry):
        acc[i] = reach(i + 4)
        return carry

    lax.fori_loop(4, 8, inner, 0)
    for e in range(2):
        sz[e, 1] = acc[4:8, 128 * e : 128 * e + 32].astype(BF)

        @pl.when(has[e])
        def _():
            send_rows(e, 1).start()

    for d in range(2):
        send_middle(d).start()
    lax.fori_loop(0, 4, inner, 0)
    lax.fori_loop(8, 12, inner, 0)

    for d in range(2):
        first = 8 - 8 * d
        for e in range(2):
            send_corner(d, e).wait_recv()
            sz[e, 2 - 2 * d] = (
                acc[first : first + 4, 128 * e : 128 * e + 32] + rxc[d, e].astype(F32)
            ).astype(BF)

            @pl.when(has[e])
            def _():
                send_rows(e, 2 - 2 * d).start()

    for d in range(2):
        send_middle(d).wait_recv()
        first = 8 - 8 * d
        acc[first : first + 4, 32:128] += rxm[d].astype(F32)

    for d in range(2):
        for part in range(3):

            @pl.when(has[1 - d])
            def _():
                send_rows(d, part).wait_recv()

    def finish(i, carry):
        factor = scale_v[i]
        part, at = i // 4, lax.rem(i, 4)
        for y in range(12):
            total = acc[i, 32 + 8 * y : 40 + 8 * y, :]
            if y >= 8:
                total += rz[0, part, at, 8 * (y - 8) : 8 * (y - 8) + 8, :].astype(F32)
            if y < 4:
                total += rz[1, part, at, 8 * y : 8 * y + 8, :].astype(F32)
            out_ref[i, y] = (factor[:, y : y + 1] * total).astype(BF)
        return carry

    lax.fori_loop(0, 12, finish, 0)

    for d in range(2):
        halo_x(d).wait_send()
        send_middle(d).wait_send()
        for e in range(2):
            send_corner(d, e).wait_send()

        @pl.when(has[d])
        def _():
            for a in range(3):
                halo_y(d, a).wait_send()
                send_rows(d, a).wait_send()
            for e in range(2):
                halo_corner(d, e).wait_send()


def fused(nx, ny, nodes, fit, xyz, idx, scale, cell, valid, radius):
    fields = nodes.shape[3]
    anywhere = pl.BlockSpec(memory_space=pl.ANY)
    scalars = pl.BlockSpec(memory_space=pltpu.SMEM)
    dma = pltpu.SemaphoreType.DMA
    return pl.pallas_call(
        functools.partial(kernel, nx, ny),
        out_shape=jax.ShapeDtypeStruct((12, 12, 8, fields), BF),
        in_specs=[anywhere] * 5 + [scalars] * 3,
        out_specs=pl.BlockSpec(memory_space=pltpu.VMEM),
        scratch_shapes=[
            pltpu.VMEM((5, 5, NSUB, fields), BF),
            pltpu.VMEM((K, PATCHES, KP), BF),
            pltpu.VMEM((3, PATCHES, K), F32),
            pltpu.VMEM((PATCHES, K), jnp.int32),
            pltpu.VMEM((12, 8, 12), F32),
            pltpu.VMEM((3, PATCHES, KL), F32),
            pltpu.VMEM((PATCHES, KS, 128), jnp.int32),
            pltpu.VMEM((3, KS * PATCHES, 128), F32),
            pltpu.VMEM((9 * SLAB, KL), BF),
            pltpu.VMEM((PATCHES, 9 * SLAB, KL), BF),
            pltpu.VMEM((PATCHES, KS, 9 * NSUB), BF),
            pltpu.VMEM((160, KL), BF),
            pltpu.VMEM((PATCHES, 10, SLAB, fields), BF),
            pltpu.VMEM((12, 160, fields), F32),
            pltpu.VMEM((2, 2, 4, 32, fields), BF),
            pltpu.VMEM((2, 4, 96, fields), BF),
            pltpu.VMEM((2, 3, 4, 32, fields), BF),
            pltpu.VMEM((2, 2, 4, 32, fields), BF),
            pltpu.VMEM((2, 4, 96, fields), BF),
            pltpu.VMEM((2, 3, 4, 32, fields), BF),
            dma((7,)),
            dma((2, 3)),
            dma((2, 3)),
            dma((2,)),
            dma((2,)),
            dma((2, 2)),
            dma((2, 2)),
            dma((2, 2)),
            dma((2, 2)),
            dma((2,)),
            dma((2,)),
            dma((2, 3)),
            dma((2, 3)),
        ],
        compiler_params=pltpu.CompilerParams(
            collective_id=0, has_side_effects=True, vmem_limit_bytes=56 * 1024 * 1024
        ),
        name="fit_and_blend",
    )(nodes, fit, xyz, idx, scale, cell, valid, radius)


def local(
    nx,
    ny,
    node_values,
    fit_ops,
    node_xyz,
    patch_nodes,
    patch_valid,
    patch_cell,
    patch_radius,
    cell_scale,
):
    return fused(
        nx,
        ny,
        node_values,
        jnp.transpose(fit_ops[0, 0], (2, 0, 1)),
        jnp.transpose(node_xyz[0, 0], (1, 0, 2)),
        patch_nodes[0, 0],
        jnp.transpose(cell_scale, (0, 2, 1)),
        jnp.transpose(patch_cell, (0, 3, 1, 2)),
        patch_valid,
        patch_radius,
    )


def solution(mesh):
    placed = (
        P("gx", "gy", None, None),
        P("gx", "gy", None, None, None),
        P("gx", "gy", None, None, None),
        P("gx", "gy", None, None),
        P("gx", "gy", None),
        P("gx", "gy", None, None),
        P("gx", "gy", None),
        P("gx", "gy", None),
    )
    return jax.shard_map(
        functools.partial(local, mesh.shape["gx"], mesh.shape["gy"]),
        mesh=mesh,
        in_specs=placed,
        out_specs=P("gx", "gy", None, None),
        check_vma=False,
    )
```

time: 120 us -> 51.6 us (0.43)
  the two profiles are of different devices: /device:TPU:87 before, /device:TPU:8 now
where the time goes in v1:
time: 51.6 us; the launch traced here: 51.4 us
  Pallas kernels  49.5 us (96%)
  local copies, waits for them, and re-layouts  1.92 us (4%)
    pallas_call x1, Pallas kernels, fused(): pl.pallas_call(functools.partial(kernel, nx, ny), out_shape=jax.ShapeDtyp...  49.5 us
    unnamed x1, local copies, waits for them, and re-layouts  1.92 us

profile of v1, /device:TPU:8, one launch (start us, length us, event | category | flops | bytes accessed | tf_op | source)
XLA Modules:
  0.0 51.4 jit_solution(11713796476067444475)
XLA Ops:
  0.0 49.5 %fit_and_blend.1 = bf16[12,12,8,256]{3,2,1,0:T(8,128)(2,1)} custom-call(bf16[3,3,128,256]{3,2,1,0:T(8,128)(2,1)} %nodes_hbm.1, bf16[300,8,320]{2,1,0:T(8,128)(2,1)} %bitcast.9, f32[3,8,300]{2,1,0:T(8,128)} %bitcast.11, s32[8,300]{1,0:T(8,128)} %bitcast.12, f32[12,8,12]{2,1,0:T(8,128)} %bitcast.10, s32[1,3,1,8]{3,2,1,0:T(1,128)} %bitcast.13, ...), custom_call_target="tpu_custom_call" | custom-call | tf_op jit(solution)/shard_map/fit_and_blend/pallas_call | solution.py:459
  49.5 1.9 %copy.10 = bf16[12,12,8,256]{3,2,1,0:T(8,128)(2,1)} copy(bf16[12,12,8,256]{3,2,1,0:T(8,128)(2,1)} %fit_and_blend.1) | data formatting | bytes 1179648

commit v2 on v1

--- a/solution.py
+++ b/solution.py
@@ -36,6 +36,7 @@
 KL = 384
 NSUB = 128
 PATCHES = 8
+RUN = 8
 SLAB = 48
 BF = jnp.bfloat16
 F32 = jnp.float32
@@ -60,9 +61,9 @@
     xyz_hbm,
     idx_hbm,
     scale_hbm,
-    cell_ref,
-    valid_ref,
-    radius_ref,
+    cell_hbm,
+    valid_hbm,
+    radius_hbm,
     out_ref,
     nbr,
     fit_v,
@@ -82,8 +83,13 @@
     sxm,
     sz,
     rxc,
+    ryc,
     rxm,
     rz,
+    out_v,
+    cell_ref,
+    valid_ref,
+    radius_ref,
     local_sem,
     hz_send,
     hz_recv,
@@ -91,16 +97,23 @@
     hx_recv,
     hf_send,
     hf_recv,
+    hg_send,
+    hg_recv,
     cc_send,
     cc_recv,
+    cy_send,
+    cy_recv,
     cm_send,
     cm_recv,
     cz_send,
     cz_recv,
+    out_sem,
 ):
     gx, gy = lax.axis_index("gx"), lax.axis_index("gy")
     left, right = lax.rem(gx + nx - 1, nx), lax.rem(gx + 1, nx)
     sides_x = (left, right)
+    far = (lax.rem(gx, RUN) == 0, lax.rem(gx, RUN) == RUN - 1)
+    near = tuple(jnp.logical_not(f) for f in far)
     has = (gy > 0, gy < ny - 1)
     sides_y = (jnp.maximum(gy - 1, 0), jnp.minimum(gy + 1, ny - 1))
 
@@ -125,6 +138,9 @@
         pltpu.make_async_copy(xyz_hbm, xyz_v, local_sem.at[1]),
         pltpu.make_async_copy(fit_hbm, fit_v, local_sem.at[2]),
         pltpu.make_async_copy(scale_hbm, scale_v, local_sem.at[3]),
+        pltpu.make_async_copy(cell_hbm, cell_ref, local_sem.at[7]),
+        pltpu.make_async_copy(valid_hbm, valid_ref, local_sem.at[8]),
+        pltpu.make_async_copy(radius_hbm, radius_ref, local_sem.at[9]),
     ]
     for a in range(3):
         fetches.append(
@@ -147,12 +163,12 @@
             sides_y[d],
         )
 
-    def halo_x(d):
-        return remote(
-            nodes_hbm.at[2 * d],
-            nbr.at[4 - 4 * d, pl.ds(1, 3)],
-            hx_send.at[d],
-            hx_recv.at[d],
+    def halo_x(d, b):
+        return remote(
+            nodes_hbm.at[2 * d, b],
+            nbr.at[4 - 4 * d, b + 1],
+            hx_send.at[d, b],
+            hx_recv.at[d, b],
             "gx",
             sides_x[d],
         )
@@ -167,6 +183,16 @@
             sides_x[d],
         )
 
+    def halo_corner_far(d, e):
+        return remote(
+            nbr.at[4 * d, 1 + 2 * e],
+            nbr.at[4 * d, 4 - 4 * e],
+            hg_send.at[d, e],
+            hg_recv.at[d, e],
+            "gy",
+            sides_y[e],
+        )
+
     for a in (0, 2, 1):
         for d in range(2):
 
@@ -174,8 +200,8 @@
             def _():
                 halo_y(d, a).start()
 
-    for d in range(2):
-        halo_x(d).start()
+        for d in range(2):
+            halo_x(d, a).start()
 
     for e in range(2):
 
@@ -185,14 +211,26 @@
                 nbr[a, 4 * e] = jnp.zeros(nbr.shape[2:], BF)
             rz[1 - e] = jnp.zeros(rz.shape[1:], BF)
 
-    fetches[0].wait()
-    fetches[1].wait()
+    for i in (0, 1, 4, 5, 6):
+        fetches[i].wait()
     xyz_p[...] = jnp.zeros(xyz_p.shape, F32)
     xyz_p[:, :, 0:K] = xyz_v[...]
-    index = jnp.concatenate(
-        [idx_v[...].astype(F32), jnp.zeros((PATCHES, KL - K), F32)], 1
+    entry = jnp.concatenate(
+        [idx_v[...], jnp.zeros((PATCHES, KL - K), jnp.int32)], 1
     )
-    columns = jnp.transpose(index)
+    sub = entry >> 7
+    a = (sub * 52) >> 8
+    patch = lax.broadcasted_iota(jnp.int32, (PATCHES, KL), 0)
+    home = jnp.zeros((PATCHES, KL), jnp.int32)
+    count = jnp.zeros((PATCHES, KL), jnp.int32)
+    for p in range(PATCHES):
+        corner = (cell_ref[0, 0, 0, p] // 4) * 3 + cell_ref[0, 1, 0, p] // 4
+        home = jnp.where(patch == p, corner, home)
+        count = jnp.where(patch == p, valid_ref[0, 0, p], count)
+    entry = ((sub - 2 * a - home) << 7) + (entry & 127)
+    slot = lax.broadcasted_iota(jnp.int32, (PATCHES, KL), 1)
+    entry = jnp.where(slot < count, entry, -1)
+    columns = jnp.transpose(entry.astype(F32))
     for p in range(PATCHES):
         idx_b[p] = jnp.broadcast_to(columns[0:KS, p : p + 1], (KS, 128)).astype(jnp.int32)
 
@@ -252,76 +290,94 @@
             return result
 
         mono_yz = powers(ey, 1) * powers(ez, 2)
-        blends = []
-        for i in range(9):
-            ex = (i - 4) * inverse
-            ex3 = jnp.concatenate([ex] * 3, 1)
-            s = (ex3 - x) * (ex3 - x) + away_yz
-            cubic = s * s * lax.rsqrt(jnp.maximum(s, 1e-30))
-            mono = powers(ex, 0) * mono_yz
-            last = jnp.where(tail < 0, cubic[:, 256:384], mono)
-            design[SLAB * i : SLAB * i + SLAB, 0:256] = cubic[:, 0:256].astype(BF)
-            design[SLAB * i : SLAB * i + SLAB, 256:384] = last.astype(BF)
-            rho = jnp.sqrt(ex * ex + flat)
-            rest = jnp.maximum(1.0 - rho, 0.0)
-            rest = rest * rest
-            blend = rest * rest * (4.0 * rho + 1.0)
-            blends.append(jnp.where(row < 36, blend, 0.0))
         ops = jnp.concatenate(
             [ops_f[t, pl.ds(p, KS, stride=8), :].astype(BF) for t in range(3)], 1
         )
         ops = jnp.concatenate([ops, jnp.zeros((KL - KS, KL), BF)], 0)
-        for i in range(9):
+        for group in range(3):
+            for i in range(3 * group, 3 * group + 3):
+                ex = (i - 4) * inverse
+                ex3 = jnp.concatenate([ex] * 3, 1)
+                s = (ex3 - x) * (ex3 - x) + away_yz
+                cubic = s * s * lax.rsqrt(jnp.maximum(s, 1e-30))
+                mono = powers(ex, 0) * mono_yz
+                last = jnp.where(tail < 0, cubic[:, 256:384], mono)
+                design[SLAB * i : SLAB * i + SLAB, 0:256] = cubic[:, 0:256].astype(BF)
+                design[SLAB * i : SLAB * i + SLAB, 256:384] = last.astype(BF)
             w = lax.dot_general(
-                design[SLAB * i : SLAB * i + SLAB, :],
+                design[3 * SLAB * group : 3 * SLAB * group + 3 * SLAB, :],
                 ops,
                 (((1,), (1,)), ((), ())),
                 preferred_element_type=F32,
             )
-            weights[p, SLAB * i : SLAB * i + SLAB, :] = (
-                w * jnp.concatenate([blends[i]] * 3, 1)
-            ).astype(BF)
+            for j in range(3):
+                i = 3 * group + j
+                ex = (i - 4) * inverse
+                rho = jnp.sqrt(ex * ex + flat)
+                rest = jnp.maximum(1.0 - rho, 0.0)
+                rest = rest * rest
+                blend = rest * rest * (4.0 * rho + 1.0)
+                blend = jnp.where(row < 36, blend, 0.0)
+                weights[p, SLAB * i : SLAB * i + SLAB, :] = (
+                    w[SLAB * j : SLAB * j + SLAB] * jnp.concatenate([blend] * 3, 1)
+                ).astype(BF)
 
         entry = idx_b[p]
-        sub = entry >> 7
-        node = entry & 127
-        a = (sub * 52) >> 8
-        b = sub - 5 * a
-        home = (cell_ref[0, 0, 0, p] // 4) * 3 + cell_ref[0, 1, 0, p] // 4
-        block = a * 3 + b - home
-        slot = lax.broadcasted_iota(jnp.int32, (KS, 128), 0)
-        block = jnp.where(slot < valid_ref[0, 0, p], block, -1)
-        match = jnp.where(
-            node == lax.broadcasted_iota(jnp.int32, (KS, 128), 1), block, -1
-        )
+        node = (entry & 127).astype(F32).astype(BF)
+        block = (entry >> 7).astype(F32).astype(BF)
+        lanes = lax.broadcasted_iota(jnp.int32, (KS, 128), 1).astype(F32).astype(BF)
+        match = jnp.where(node == lanes, block, jnp.full((KS, 128), -1.0, BF))
+        one, zero = jnp.full((KS, 128), 1.0, BF), jnp.zeros((KS, 128), BF)
         for t in range(9):
-            onehot[p, :, 128 * t : 128 * t + 128] = jnp.where(match == t, 1.0, 0.0).astype(BF)
+            onehot[p, :, 128 * t : 128 * t + 128] = jnp.where(
+                match == jnp.full((KS, 128), t, BF), one, zero
+            )
         return carry
 
     lax.fori_loop(0, 4, prepare, 0)
     for e in range(2):
-
-        @pl.when(has[e])
-        def _():
-            for d in range(2):
+        for d in range(2):
+
+            @pl.when(has[e] & near[d])
+            def _():
                 halo_y(1 - e, 2 * d).wait_recv()
                 halo_corner(e, d).start()
 
+            @pl.when(has[e] & far[d])
+            def _():
+                halo_x(1 - d, 2 * e).wait_recv()
+                halo_corner_far(d, e).start()
+
     lax.fori_loop(4, PATCHES, prepare, 0)
 
-    for fetch in fetches[3:]:
-        fetch.wait()
-    for d in range(2):
-        halo_x(d).wait_recv()
+    for i in (3, 7, 8, 9):
+        fetches[i].wait()
+    for d in range(2):
+        halo_x(d, 1).wait_recv()
+        for e in range(2):
+            @pl.when(near[1 - d] | jnp.logical_not(has[e]))
+            def _():
+                halo_x(d, 2 * e).wait_recv()
+
+            @pl.when(has[e] & far[d])
+            def _():
+                halo_y(1 - e, 2 * d).wait_recv()
+
+            @pl.when(has[e] & near[d])
+            def _():
+                halo_corner(e, 1 - d).wait_recv()
+
+            @pl.when(has[e] & far[d])
+            def _():
+                halo_corner_far(d, 1 - e).wait_recv()
+
     for e in range(2):
 
         @pl.when(has[e])
         def _():
             halo_y(1 - e, 1).wait_recv()
-            for d in range(2):
-                halo_corner(e, d).wait_recv()
-
-    def values(p, carry):
+
+    for p in range(PATCHES):
         home_x, home_y = cell_ref[0, 0, 0, p] // 4, cell_ref[0, 1, 0, p] // 4
         window = jnp.concatenate(
             [
@@ -336,9 +392,6 @@
         )
         terms = jnp.dot(weights[p], samples, preferred_element_type=F32).astype(BF)
         slabs[p, 0:9] = terms.reshape(9, SLAB, terms.shape[1])
-        return carry
-
-    lax.fori_loop(0, PATCHES, values, 0)
 
     def reach(x):
         parts = []
@@ -355,8 +408,20 @@
             sxc.at[d, e], rxc.at[d, e], cc_send.at[d, e], cc_recv.at[d, e], "gx", sides_x[d]
         )
 
-    def send_middle(d):
-        return remote(sxm.at[d], rxm.at[d], cm_send.at[d], cm_recv.at[d], "gx", sides_x[d])
+    def send_corner_far(d, e):
+        return remote(
+            sxc.at[d, e], ryc.at[d, e], cy_send.at[d, e], cy_recv.at[d, e], "gy", sides_y[e]
+        )
+
+    def send_middle(d, part):
+        return remote(
+            sxm.at[d, part],
+            rxm.at[d, part],
+            cm_send.at[d, part],
+            cm_recv.at[d, part],
+            "gx",
+            sides_x[d],
+        )
 
     def send_rows(d, part):
         return remote(
@@ -369,23 +434,36 @@
         )
 
     for d in range(2):
-
-        def outer(i, carry):
+        for i in range(4):
             row = reach(16 * d + i)
             sxc[d, 0, i] = row[0:32].astype(BF)
-            sxm[d, i] = row[32:128].astype(BF)
+            for part in range(3):
+                sxm[d, part, i] = row[32 + 32 * part : 64 + 32 * part].astype(BF)
             sxc[d, 1, i] = row[128:160].astype(BF)
-            return carry
-
-        lax.fori_loop(0, 4, outer, 0)
+
+        @pl.when(near[d])
+        def _():
+            for e in range(2):
+                send_corner(d, e).start()
+            for part in range(3):
+                send_middle(d, part).start()
+
         for e in range(2):
-            send_corner(d, e).start()
-
-    def inner(i, carry):
+
+            @pl.when(far[d] & has[e])
+            def _():
+                send_corner_far(d, e).start()
+
+            @pl.when(far[d] & jnp.logical_not(has[e]))
+            def _():
+                send_middle(d, 2 * e).start()
+
+        @pl.when(far[d])
+        def _():
+            send_middle(d, 1).start()
+
+    for i in range(4, 8):
         acc[i] = reach(i + 4)
-        return carry
-
-    lax.fori_loop(4, 8, inner, 0)
     for e in range(2):
         sz[e, 1] = acc[4:8, 128 * e : 128 * e + 32].astype(BF)
 
@@ -393,34 +471,58 @@
         def _():
             send_rows(e, 1).start()
 
-    for d in range(2):
-        send_middle(d).start()
-    lax.fori_loop(0, 4, inner, 0)
-    lax.fori_loop(8, 12, inner, 0)
+    for i in (0, 1, 2, 3, 8, 9, 10, 11):
+        acc[i] = reach(i + 4)
+
+    for d in range(2):
+        for e in range(2):
+
+            @pl.when(far[d] & has[e])
+            def _():
+                send_corner_far(d, 1 - e).wait_recv()
+                sxm[d, 2 * e] = (
+                    sxm[d, 2 * e].astype(F32) + ryc[d, 1 - e].astype(F32)
+                ).astype(BF)
+                send_middle(d, 2 * e).start()
 
     for d in range(2):
         first = 8 - 8 * d
+
+        @pl.when(far[1 - d])
+        def _():
+            for e in range(2):
+                sz[e, 2 - 2 * d] = acc[first : first + 4, 128 * e : 128 * e + 32].astype(BF)
+
+        @pl.when(near[1 - d])
+        def _():
+            for e in range(2):
+                send_corner(d, e).wait_recv()
+                sz[e, 2 - 2 * d] = (
+                    acc[first : first + 4, 128 * e : 128 * e + 32] + rxc[d, e].astype(F32)
+                ).astype(BF)
+
         for e in range(2):
-            send_corner(d, e).wait_recv()
-            sz[e, 2 - 2 * d] = (
-                acc[first : first + 4, 128 * e : 128 * e + 32] + rxc[d, e].astype(F32)
-            ).astype(BF)
 
             @pl.when(has[e])
             def _():
                 send_rows(e, 2 - 2 * d).start()
 
     for d in range(2):
-        send_middle(d).wait_recv()
         first = 8 - 8 * d
-        acc[first : first + 4, 32:128] += rxm[d].astype(F32)
-
-    for d in range(2):
         for part in range(3):
+            send_middle(d, part).wait_recv()
+            at = 32 + 32 * part
+            acc[first : first + 4, at : at + 32] += rxm[d, part].astype(F32)
+
+    for d in range(2):
+        for part in range(3):
 
             @pl.when(has[1 - d])
             def _():
                 send_rows(d, part).wait_recv()
+
+    def leave(i):
+        return pltpu.make_async_copy(out_v.at[i], out_ref.at[i], out_sem.at[i])
 
     def finish(i, carry):
         factor = scale_v[i]
@@ -431,36 +533,51 @@
                 total += rz[0, part, at, 8 * (y - 8) : 8 * (y - 8) + 8, :].astype(F32)
             if y < 4:
                 total += rz[1, part, at, 8 * y : 8 * y + 8, :].astype(F32)
-            out_ref[i, y] = (factor[:, y : y + 1] * total).astype(BF)
+            out_v[i, y] = (factor[:, y : y + 1] * total).astype(BF)
+        leave(i).start()
         return carry
 
     lax.fori_loop(0, 12, finish, 0)
 
-    for d in range(2):
-        halo_x(d).wait_send()
-        send_middle(d).wait_send()
+    for i in range(12):
+        leave(i).wait()
+    for d in range(2):
+        for part in range(3):
+            halo_x(d, part).wait_send()
+            send_middle(d, part).wait_send()
+
+        @pl.when(near[d])
+        def _():
+            for e in range(2):
+                send_corner(d, e).wait_send()
+
         for e in range(2):
-            send_corner(d, e).wait_send()
+
+            @pl.when(has[e] & near[d])
+            def _():
+                halo_corner(e, d).wait_send()
+
+            @pl.when(has[e] & far[d])
+            def _():
+                halo_corner_far(d, e).wait_send()
+                send_corner_far(d, e).wait_send()
 
         @pl.when(has[d])
         def _():
             for a in range(3):
                 halo_y(d, a).wait_send()
                 send_rows(d, a).wait_send()
-            for e in range(2):
-                halo_corner(d, e).wait_send()
 
 
 def fused(nx, ny, nodes, fit, xyz, idx, scale, cell, valid, radius):
     fields = nodes.shape[3]
     anywhere = pl.BlockSpec(memory_space=pl.ANY)
-    scalars = pl.BlockSpec(memory_space=pltpu.SMEM)
     dma = pltpu.SemaphoreType.DMA
     return pl.pallas_call(
         functools.partial(kernel, nx, ny),
         out_shape=jax.ShapeDtypeStruct((12, 12, 8, fields), BF),
-        in_specs=[anywhere] * 5 + [scalars] * 3,
-        out_specs=pl.BlockSpec(memory_space=pltpu.VMEM),
+        in_specs=[anywhere] * 8,
+        out_specs=anywhere,
         scratch_shapes=[
             pltpu.VMEM((5, 5, NSUB, fields), BF),
             pltpu.VMEM((K, PATCHES, KP), BF),
@@ -477,24 +594,34 @@
             pltpu.VMEM((PATCHES, 10, SLAB, fields), BF),
             pltpu.VMEM((12, 160, fields), F32),
             pltpu.VMEM((2, 2, 4, 32, fields), BF),
-            pltpu.VMEM((2, 4, 96, fields), BF),
+            pltpu.VMEM((2, 3, 4, 32, fields), BF),
             pltpu.VMEM((2, 3, 4, 32, fields), BF),
             pltpu.VMEM((2, 2, 4, 32, fields), BF),
-            pltpu.VMEM((2, 4, 96, fields), BF),
+            pltpu.VMEM((2, 2, 4, 32, fields), BF),
             pltpu.VMEM((2, 3, 4, 32, fields), BF),
-            dma((7,)),
-            dma((2, 3)),
-            dma((2, 3)),
-            dma((2,)),
-            dma((2,)),
-            dma((2, 2)),
-            dma((2, 2)),
-            dma((2, 2)),
-            dma((2, 2)),
-            dma((2,)),
-            dma((2,)),
-            dma((2, 3)),
-            dma((2, 3)),
+            pltpu.VMEM((2, 3, 4, 32, fields), BF),
+            pltpu.VMEM((12, 12, 8, fields), BF),
+            pltpu.SMEM((1, 3, 1, PATCHES), jnp.int32),
+            pltpu.SMEM((1, 1, PATCHES), jnp.int32),
+            pltpu.SMEM((1, 1, PATCHES), F32),
+            dma((10,)),
+            dma((2, 3)),
+            dma((2, 3)),
+            dma((2, 3)),
+            dma((2, 3)),
+            dma((2, 2)),
+            dma((2, 2)),
+            dma((2, 2)),
+            dma((2, 2)),
+            dma((2, 2)),
+            dma((2, 2)),
+            dma((2, 2)),
+            dma((2, 2)),
+            dma((2, 3)),
+            dma((2, 3)),
+            dma((2, 3)),
+            dma((2, 3)),
+            dma((12,)),
         ],
         compiler_params=pltpu.CompilerParams(
             collective_id=0, has_side_effects=True, vmem_limit_bytes=56 * 1024 * 1024

time: 51.6 us -> 47.4 us (0.919)
  Pallas kernels: 49.5 us -> 45.3 us
    pallas_call x1, Pallas kernels: 49.5 us -> 45.3 us  [fused(): pl.pallas_call(functools.partial(kernel, nx, ny), out_shape=jax.ShapeDtyp...]
where the time goes in v2:
time: 47.4 us; the launch traced here: 47.2 us
  Pallas kernels  45.3 us (96%)
  local copies, waits for them, and re-layouts  1.92 us (4%)
    pallas_call x1, Pallas kernels, fused(): pl.pallas_call(functools.partial(kernel, nx, ny), out_shape=jax.ShapeDtyp...  45.3 us
    unnamed x1, local copies, waits for them, and re-layouts  1.92 us

profile of v2, /device:TPU:8, one launch (start us, length us, event | category | flops | bytes accessed | tf_op | source)
XLA Modules:
  0.0 47.2 jit_solution(6543065811947895040)
XLA Ops:
  0.0 45.3 %fit_and_blend.1 = bf16[12,12,8,256]{3,2,1,0:T(8,128)(2,1)} custom-call(bf16[3,3,128,256]{3,2,1,0:T(8,128)(2,1)} %nodes_hbm.1, bf16[300,8,320]{2,1,0:T(8,128)(2,1)} %bitcast.9, f32[3,8,300]{2,1,0:T(8,128)} %bitcast.11, s32[8,300]{1,0:T(8,128)} %bitcast.12, f32[12,8,12]{2,1,0:T(8,128)} %bitcast.10, s32[1,3,1,8]{3,2,1,0:T(1,128)} %bitcast.13, ...), custom_call_target="tpu_custom_call" | custom-call | tf_op jit(solution)/shard_map/fit_and_blend/pallas_call | solution.py:576
  45.3 1.9 %copy.10 = bf16[12,12,8,256]{3,2,1,0:T(8,128)(2,1)} copy(bf16[12,12,8,256]{3,2,1,0:T(8,128)(2,1)} %fit_and_blend.1) | data formatting | bytes 1179648

commit v3 on v2

--- a/solution.py
+++ b/solution.py
@@ -77,6 +77,7 @@
     weights,
     onehot,
     place,
+    samples,
     slabs,
     acc,
     sxc,
@@ -133,29 +134,31 @@
                 device_id_type=pl.DeviceIdType.MESH,
             )
 
+    own = [
+        pltpu.make_async_copy(
+            nodes_hbm.at[a], nbr.at[a + 1, pl.ds(1, 3)], local_sem.at[7 + a]
+        )
+        for a in range(3)
+    ]
     fetches = [
         pltpu.make_async_copy(idx_hbm, idx_v, local_sem.at[0]),
         pltpu.make_async_copy(xyz_hbm, xyz_v, local_sem.at[1]),
         pltpu.make_async_copy(fit_hbm, fit_v, local_sem.at[2]),
         pltpu.make_async_copy(scale_hbm, scale_v, local_sem.at[3]),
-        pltpu.make_async_copy(cell_hbm, cell_ref, local_sem.at[7]),
-        pltpu.make_async_copy(valid_hbm, valid_ref, local_sem.at[8]),
-        pltpu.make_async_copy(radius_hbm, radius_ref, local_sem.at[9]),
+        pltpu.make_async_copy(cell_hbm, cell_ref, local_sem.at[4]),
+        pltpu.make_async_copy(valid_hbm, valid_ref, local_sem.at[5]),
+        pltpu.make_async_copy(radius_hbm, radius_ref, local_sem.at[6]),
     ]
-    for a in range(3):
-        fetches.append(
-            pltpu.make_async_copy(
-                nodes_hbm.at[a], nbr.at[a + 1, pl.ds(1, 3)], local_sem.at[4 + a]
-            )
-        )
-    for fetch in fetches:
+    for fetch in own + fetches:
         fetch.start()
+    for fetch in own:
+        fetch.wait()
     waits = 2 + jnp.where(gy > 0, 1, 0) + jnp.where(gy < ny - 1, 1, 0)
     pl.semaphore_wait(barrier, waits)
 
     def halo_y(d, a):
         return remote(
-            nodes_hbm.at[a, 2 * d],
+            nbr.at[a + 1, 1 + 2 * d],
             nbr.at[a + 1, 4 - 4 * d],
             hz_send.at[d, a],
             hz_recv.at[d, a],
@@ -165,7 +168,7 @@
 
     def halo_x(d, b):
         return remote(
-            nodes_hbm.at[2 * d, b],
+            nbr.at[1 + 2 * d, b + 1],
             nbr.at[4 - 4 * d, b + 1],
             hx_send.at[d, b],
             hx_recv.at[d, b],
@@ -236,6 +239,7 @@
 
     for p in range(PATCHES):
         slabs[p, 9] = jnp.zeros((SLAB, slabs.shape[3]), BF)
+        samples[p, KS:KL] = jnp.zeros((KL - KS, samples.shape[2]), BF)
 
     lane = lax.broadcasted_iota(jnp.int32, (1, KL), 1)
     owner, within = lane // SLAB, lane % SLAB
@@ -350,8 +354,7 @@
 
     lax.fori_loop(4, PATCHES, prepare, 0)
 
-    for i in (3, 7, 8, 9):
-        fetches[i].wait()
+    fetches[3].wait()
     for d in range(2):
         halo_x(d, 1).wait_recv()
         for e in range(2):
@@ -386,12 +389,18 @@
             ],
             0,
         )
-        samples = jnp.dot(onehot[p], window, preferred_element_type=F32).astype(BF)
-        samples = jnp.concatenate(
-            [samples, jnp.zeros((KL - KS, samples.shape[1]), BF)], 0
-        )
-        terms = jnp.dot(weights[p], samples, preferred_element_type=F32).astype(BF)
-        slabs[p, 0:9] = terms.reshape(9, SLAB, terms.shape[1])
+        samples[p, 0:KS] = jnp.dot(
+            onehot[p], window, preferred_element_type=F32
+        ).astype(BF)
+
+    def evaluate(i, carry):
+        for j in range(4):
+            p = 4 * i + j
+            terms = jnp.dot(weights[p], samples[p], preferred_element_type=F32)
+            slabs[p, 0:9] = terms.astype(BF).reshape(9, SLAB, terms.shape[1])
+        return carry
+
+    lax.fori_loop(0, 2, evaluate, 0)
 
     def reach(x):
         parts = []
@@ -507,37 +516,38 @@
             def _():
                 send_rows(e, 2 - 2 * d).start()
 
-    for d in range(2):
-        first = 8 - 8 * d
-        for part in range(3):
-            send_middle(d, part).wait_recv()
-            at = 32 + 32 * part
-            acc[first : first + 4, at : at + 32] += rxm[d, part].astype(F32)
-
-    for d in range(2):
-        for part in range(3):
-
-            @pl.when(has[1 - d])
-            def _():
-                send_rows(d, part).wait_recv()
-
     def leave(i):
         return pltpu.make_async_copy(out_v.at[i], out_ref.at[i], out_sem.at[i])
 
-    def finish(i, carry):
-        factor = scale_v[i]
-        part, at = i // 4, lax.rem(i, 4)
-        for y in range(12):
-            total = acc[i, 32 + 8 * y : 40 + 8 * y, :]
-            if y >= 8:
-                total += rz[0, part, at, 8 * (y - 8) : 8 * (y - 8) + 8, :].astype(F32)
-            if y < 4:
-                total += rz[1, part, at, 8 * y : 8 * y + 8, :].astype(F32)
-            out_v[i, y] = (factor[:, y : y + 1] * total).astype(BF)
-        leave(i).start()
-        return carry
-
-    lax.fori_loop(0, 12, finish, 0)
+    def finish(part, d):
+        def one(at, carry):
+            i = 4 * part + at
+            factor = scale_v[i]
+            for y in range(12):
+                total = acc[i, 32 + 8 * y : 40 + 8 * y, :]
+                third, row = y // 4, 8 * (y % 4)
+                if d is not None:
+                    total += rxm[d, third, at, row : row + 8, :].astype(F32)
+                if third != 1:
+                    total += rz[1 - third // 2, part, at, row : row + 8, :].astype(F32)
+                out_v[i, y] = (factor[:, y : y + 1] * total).astype(BF)
+            leave(i).start()
+            return carry
+
+        for e in range(2):
+
+            @pl.when(has[1 - e])
+            def _():
+                send_rows(e, part).wait_recv()
+
+        if d is not None:
+            for third in range(3):
+                send_middle(d, third).wait_recv()
+        lax.fori_loop(0, 4, one, 0)
+
+    finish(1, None)
+    finish(0, 1)
+    finish(2, 0)
 
     for i in range(12):
         leave(i).wait()
@@ -591,6 +601,7 @@
             pltpu.VMEM((PATCHES, 9 * SLAB, KL), BF),
             pltpu.VMEM((PATCHES, KS, 9 * NSUB), BF),
             pltpu.VMEM((160, KL), BF),
+            pltpu.VMEM((PATCHES, KL, fields), BF),
             pltpu.VMEM((PATCHES, 10, SLAB, fields), BF),
             pltpu.VMEM((12, 160, fields), F32),
             pltpu.VMEM((2, 2, 4, 32, fields), BF),

time: 47.4 us -> 44.3 us (0.935)
  Pallas kernels: 45.3 us -> 42.1 us
    pallas_call x1, Pallas kernels: 45.3 us -> 42.1 us  [fused(): pl.pallas_call(functools.partial(kernel, nx, ny), out_shape=jax.ShapeDtyp...]
where the time goes in v3:
time: 44.3 us; the launch traced here: 44.1 us
  Pallas kernels  42.1 us (95%)
  local copies, waits for them, and re-layouts  1.92 us (4%)
    pallas_call x1, Pallas kernels, fused(): pl.pallas_call(functools.partial(kernel, nx, ny), out_shape=jax.ShapeDtyp...  42.1 us
    unnamed x1, local copies, waits for them, and re-layouts  1.92 us

profile of v3, /device:TPU:8, one launch (start us, length us, event | category | flops | bytes accessed | tf_op | source)
XLA Modules:
  0.0 44.1 jit_solution(6842708902982344495)
XLA Ops:
  0.0 42.1 %fit_and_blend.1 = bf16[12,12,8,256]{3,2,1,0:T(8,128)(2,1)} custom-call(bf16[3,3,128,256]{3,2,1,0:T(8,128)(2,1)} %nodes_hbm.1, bf16[300,8,320]{2,1,0:T(8,128)(2,1)} %bitcast.9, f32[3,8,300]{2,1,0:T(8,128)} %bitcast.11, s32[8,300]{1,0:T(8,128)} %bitcast.12, f32[12,8,12]{2,1,0:T(8,128)} %bitcast.10, s32[1,3,1,8]{3,2,1,0:T(1,128)} %bitcast.13, ...), custom_call_target="tpu_custom_call" | custom-call | tf_op jit(solution)/shard_map/fit_and_blend/pallas_call | solution.py:586
  42.1 1.9 %copy.10 = bf16[12,12,8,256]{3,2,1,0:T(8,128)(2,1)} copy(bf16[12,12,8,256]{3,2,1,0:T(8,128)(2,1)} %fit_and_blend.1) | data formatting | bytes 1179648

commit v4 on v3

--- a/solution.py
+++ b/solution.py
@@ -91,6 +91,7 @@
     cell_ref,
     valid_ref,
     radius_ref,
+    ready,
     local_sem,
     hz_send,
     hz_recv,
@@ -119,10 +120,16 @@
     sides_y = (jnp.maximum(gy - 1, 0), jnp.minimum(gy + 1, ny - 1))
 
     barrier = pltpu.get_barrier_semaphore()
-    for side in sides_x:
+    pl.semaphore_signal(
+        barrier, inc=1, device_id={"gx": left}, device_id_type=pl.DeviceIdType.MESH
+    )
+
+    @pl.when(near[1])
+    def _():
         pl.semaphore_signal(
-            barrier, inc=1, device_id={"gx": side}, device_id_type=pl.DeviceIdType.MESH
-        )
+            barrier, inc=1, device_id={"gx": right}, device_id_type=pl.DeviceIdType.MESH
+        )
+
     for d in range(2):
 
         @pl.when(has[d])
@@ -151,10 +158,19 @@
     ]
     for fetch in own + fetches:
         fetch.start()
+    waits = 1 + jnp.where(near[0], 1, 0)
+    waits += jnp.where(gy > 0, 1, 0) + jnp.where(gy < ny - 1, 1, 0)
+    pl.semaphore_wait(barrier, waits)
+
+    @pl.when(far[1])
+    def _():
+        pl.semaphore_signal(
+            ready, inc=1, device_id={"gx": right}, device_id_type=pl.DeviceIdType.MESH
+        )
+
     for fetch in own:
         fetch.wait()
-    waits = 2 + jnp.where(gy > 0, 1, 0) + jnp.where(gy < ny - 1, 1, 0)
-    pl.semaphore_wait(barrier, waits)
+
 
     def halo_y(d, a):
         return remote(
@@ -203,8 +219,12 @@
             def _():
                 halo_y(d, a).start()
 
-        for d in range(2):
-            halo_x(d, a).start()
+        halo_x(1, a).start()
+
+        @pl.when(near[0])
+        def _():
+            halo_x(0, a).start()
+
 
     for e in range(2):
 
@@ -338,7 +358,15 @@
             )
         return carry
 
-    lax.fori_loop(0, 4, prepare, 0)
+    lax.fori_loop(0, 5, prepare, 0)
+
+    @pl.when(far[0])
+    def _():
+        pl.semaphore_wait(ready, 1)
+        for a in (0, 2, 1):
+            halo_x(0, a).start()
+
+    lax.fori_loop(5, 6, prepare, 0)
     for e in range(2):
         for d in range(2):
 
@@ -347,12 +375,14 @@
                 halo_y(1 - e, 2 * d).wait_recv()
                 halo_corner(e, d).start()
 
+    lax.fori_loop(6, PATCHES, prepare, 0)
+    for e in range(2):
+        for d in range(2):
+
             @pl.when(has[e] & far[d])
             def _():
                 halo_x(1 - d, 2 * e).wait_recv()
                 halo_corner_far(d, e).start()
-
-    lax.fori_loop(4, PATCHES, prepare, 0)
 
     fetches[3].wait()
     for d in range(2):
@@ -484,6 +514,15 @@
         acc[i] = reach(i + 4)
 
     for d in range(2):
+        first = 8 - 8 * d
+        for e in range(2):
+
+            @pl.when(has[e] & far[1 - d])
+            def _():
+                sz[e, 2 - 2 * d] = acc[first : first + 4, 128 * e : 128 * e + 32].astype(BF)
+                send_rows(e, 2 - 2 * d).start()
+
+    for d in range(2):
         for e in range(2):
 
             @pl.when(far[d] & has[e])
@@ -497,11 +536,6 @@
     for d in range(2):
         first = 8 - 8 * d
 
-        @pl.when(far[1 - d])
-        def _():
-            for e in range(2):
-                sz[e, 2 - 2 * d] = acc[first : first + 4, 128 * e : 128 * e + 32].astype(BF)
-
         @pl.when(near[1 - d])
         def _():
             for e in range(2):
@@ -512,7 +546,7 @@
 
         for e in range(2):
 
-            @pl.when(has[e])
+            @pl.when(has[e] & near[1 - d])
             def _():
                 send_rows(e, 2 - 2 * d).start()
 
@@ -615,6 +649,7 @@
             pltpu.SMEM((1, 3, 1, PATCHES), jnp.int32),
             pltpu.SMEM((1, 1, PATCHES), jnp.int32),
             pltpu.SMEM((1, 1, PATCHES), F32),
+            pltpu.SemaphoreType.REGULAR,
             dma((10,)),
             dma((2, 3)),
             dma((2, 3)),

time: 44.3 us -> 44 us (level)
  no operation moved by 1% of the time
where the time goes in v4:
time: 44 us; the launch traced here: 43.8 us
  Pallas kernels  41.9 us (95%)
  local copies, waits for them, and re-layouts  1.92 us (4%)
    pallas_call x1, Pallas kernels, fused(): pl.pallas_call(functools.partial(kernel, nx, ny), out_shape=jax.ShapeDtyp...  41.9 us
    unnamed x1, local copies, waits for them, and re-layouts  1.92 us

profile of v4, /device:TPU:8, one launch (start us, length us, event | category | flops | bytes accessed | tf_op | source)
XLA Modules:
  0.0 43.8 jit_solution(6024687957353681531)
XLA Ops:
  0.0 41.9 %fit_and_blend.1 = bf16[12,12,8,256]{3,2,1,0:T(8,128)(2,1)} custom-call(bf16[3,3,128,256]{3,2,1,0:T(8,128)(2,1)} %nodes_hbm.1, bf16[300,8,320]{2,1,0:T(8,128)(2,1)} %bitcast.9, f32[3,8,300]{2,1,0:T(8,128)} %bitcast.11, s32[8,300]{1,0:T(8,128)} %bitcast.12, f32[12,8,12]{2,1,0:T(8,128)} %bitcast.10, s32[1,3,1,8]{3,2,1,0:T(1,128)} %bitcast.13, ...), custom_call_target="tpu_custom_call" | custom-call | tf_op jit(solution)/shard_map/fit_and_blend/pallas_call | solution.py:620
  41.9 1.9 %copy.10 = bf16[12,12,8,256]{3,2,1,0:T(8,128)(2,1)} copy(bf16[12,12,8,256]{3,2,1,0:T(8,128)(2,1)} %fit_and_blend.1) | data formatting | bytes 1179648
